TPU v7x, 32 devices: a whole 2x2x4 slice. The times are simulated.
32 devices in a mesh: row: 8 (over z, x), col: 4 (over y, core).
Axes of the slice: x: 2, y: 2, z: 4, core: 2. Of those that a mesh axis runs over, the one named last changes fastest.
Arguments:
- offsets: int32 [8, 4, 2], P('row', 'col'), may hold values from 1 to 3
- targets: float32 [3, 3, 256, 512], P(None, None, 'row', 'col'), may hold values from -60 to 60
- grid_fine: float32 [32, 256, 512], P(None, 'row', 'col'), may hold values from -6 to 6
- grid_coarse: float32 [32, 64, 128], P(None, 'row', 'col'), may hold values from -6 to 6
- weight_in: float32 [512, 64], replicated, may hold values from -0.75 to 0.75
- weight_mid: float32 [1, 512, 512], replicated, may hold values from -0.25 to 0.25
- weight_out: float32 [3, 512], replicated, may hold values from -0.397747564 to 0.397747564
- fine_first: float32 [32, 256, 512], P(None, 'row', 'col'), may hold values from -0.012 to 0.012
- fine_second: float32 [32, 256, 512], P(None, 'row', 'col'), may hold values from 1e-06 to 0.0001
- coarse_first: float32 [32, 64, 128], P(None, 'row', 'col'), may hold values from -0.012 to 0.012
- coarse_second: float32 [32, 64, 128], P(None, 'row', 'col'), may hold values from 1e-06 to 0.0001
- in_first: float32 [512, 64], replicated, may hold values from -0.012 to 0.012
- in_second: float32 [512, 64], replicated, may hold values from 1e-06 to 0.0001
- mid_first: float32 [1, 512, 512], replicated, may hold values from -0.012 to 0.012
- mid_second: float32 [1, 512, 512], replicated, may hold values from 1e-06 to 0.0001
- out_first: float32 [3, 512], replicated, may hold values from -0.012 to 0.012
- out_second: float32 [3, 512], replicated, may hold values from 1e-06 to 0.0001
Outputs:
- fine_step: float32 [32, 256, 512], P(None, 'row', 'col')
- coarse_step: float32 [32, 64, 128], P(None, 'row', 'col')
- input_step: float32 [512, 64], replicated
- middle_step: float32 [1, 512, 512], replicated
- output_step: float32 [3, 512], replicated
All inputs are finite; a program needn't handle non-finite values.
Results may differ from a plain program's by a relative error of at most 0.0014.
The roundings to bfloat16 on the way count: a program that leaves them out, or rounds other values in their place, can miss the bound.
Values sent between devices are 32-bit elements; how exact they have to be, the bound alone decides.
A program may use at most 64 MiB of HBM per device.

v0:
```python
import jax
import jax.numpy as jnp
from jax import lax
from jax.sharding import PartitionSpec as P

SUB = 4
RATIO = 4
ADAM_STEP = 10
BETA_ONE = 0.9
BETA_TWO = 0.99
ADAM_EPSILON = 1e-08
CLIP_RMS = 0.01
LOSS_VALUE = 0.25
MEAN_EPSILON = 1e-06


def shifted(block, axis, distance):
    devices = range(lax.axis_size(axis))
    route = [(i - distance, i) for i in devices if i - distance in devices]
    return lax.ppermute(block, axis, route)


def interp_table(samples, level_ratio, offset):
    positions = jnp.arange(samples, dtype=jnp.int32)
    base_index = positions // level_ratio
    fraction = (
        (positions % level_ratio).astype(jnp.float32) + offset.astype(jnp.float32) / SUB
    ) / level_ratio
    column = jnp.arange(samples // level_ratio + 1, dtype=jnp.int32)
    lower_hit = (column[None, :] == base_index[:, None]).astype(jnp.float32)
    upper_hit = (column[None, :] == base_index[:, None] + 1).astype(jnp.float32)
    return lower_hit * (1.0 - fraction)[:, None] + upper_hit * fraction[:, None]


def level_tables(row_count, col_count, shift_y, shift_x):
    return (
        interp_table(row_count, 1, shift_y),
        interp_table(col_count, 1, shift_x),
        interp_table(row_count, RATIO, shift_y),
        interp_table(col_count, RATIO, shift_x),
    )


def sample_level(extended, row_table, col_table):
    across = jnp.einsum("kjl,ml->kjm", extended, col_table, precision=lax.Precision.HIGHEST)
    return jnp.einsum("ij,kjm->kim", row_table, across, precision=lax.Precision.HIGHEST)


def spread_level(cotangent, row_table, col_table):
    backward = jnp.einsum("ij,kim->kjm", row_table, cotangent, precision=lax.Precision.HIGHEST)
    return jnp.einsum("kjm,ml->kjl", backward, col_table, precision=lax.Precision.HIGHEST)


def sample_features(fine_ext, coarse_ext, tables):
    fine_feat = sample_level(fine_ext, tables[0], tables[1])
    coarse_feat = sample_level(coarse_ext, tables[2], tables[3])
    channels, row_count, col_count = fine_feat.shape
    return jnp.concatenate(
        [
            fine_feat.reshape(channels, row_count * col_count),
            coarse_feat.reshape(channels, row_count * col_count),
        ],
        axis=0,
    ).astype(jnp.bfloat16)


def spread_features(feature_grad, tables):
    channels = feature_grad.shape[0] // 2
    row_count = tables[0].shape[0]
    col_count = tables[1].shape[0]
    fine_cot = feature_grad[:channels].reshape(channels, row_count, col_count)
    coarse_cot = feature_grad[channels:].reshape(channels, row_count, col_count)
    return (
        spread_level(fine_cot, tables[0], tables[1]),
        spread_level(coarse_cot, tables[2], tables[3]),
    )


def matmul(former, latter):
    return jnp.dot(former, latter, preferred_element_type=jnp.float32)


def contract_rows(former, latter):
    return lax.dot_general(
        former, latter, (((0,), (0,)), ((), ())), preferred_element_type=jnp.float32
    )


def contract_cols(former, latter):
    return lax.dot_general(
        former, latter, (((1,), (1,)), ((), ())), preferred_element_type=jnp.float32
    )


def silu_slope(pre_act):
    sigmoid = jax.nn.sigmoid(pre_act)
    return sigmoid * (1.0 + pre_act * (1.0 - sigmoid))


def decoder_forward(features, low_in, low_mid, low_out):
    pre_acts = [matmul(low_in, features)]
    activations = [jax.nn.silu(pre_acts[0]).astype(jnp.bfloat16)]
    pre_acts.append(matmul(low_mid[0], activations[-1]))
    activations.append(jax.nn.silu(pre_acts[-1]).astype(jnp.bfloat16))
    return (matmul(low_out, activations[-1]), pre_acts, activations)


def decoder_backward(features, pre_acts, activations, cotangent, low_in, low_mid, low_out):
    out_cotangent = cotangent.astype(jnp.bfloat16)
    grad_out = contract_cols(out_cotangent, activations[-1])
    upward = contract_rows(low_out, out_cotangent)
    grads_mid = []
    delta_low = (upward * silu_slope(pre_acts[1])).astype(jnp.bfloat16)
    grads_mid.insert(0, contract_cols(delta_low, activations[0]))
    upward = contract_rows(low_mid[0], delta_low)
    delta_low = (upward * silu_slope(pre_acts[0])).astype(jnp.bfloat16)
    grad_in = contract_cols(delta_low, features)
    feature_grad = contract_rows(low_in, delta_low)
    return (grad_in, jnp.stack(grads_mid), grad_out, feature_grad)


def pixel_cotangent(value_error, row_error, row_prior, col_error, col_prior):
    return (
        2.0 * LOSS_VALUE * value_error
        + 2.0 * (row_prior - row_error)
        + 2.0 * (col_prior - col_error)
    )


def clip_factor(total, entries):
    return jnp.minimum(1.0, CLIP_RMS / jnp.sqrt(total / entries + MEAN_EPSILON))


def adam_step(gradient, moment_one, moment_two, clip_scale):
    clipped = gradient * clip_scale
    new_one = BETA_ONE * moment_one + (1.0 - BETA_ONE) * clipped
    new_two = BETA_TWO * moment_two + (1.0 - BETA_TWO) * clipped * clipped
    return (
        new_one
        / (1.0 - BETA_ONE**ADAM_STEP)
        / (jnp.sqrt(new_two / (1.0 - BETA_TWO**ADAM_STEP)) + ADAM_EPSILON)
    )


def grid_total_sum(grid_local):
    return lax.psum(grid_local, ("row", "col"))


def shards(
    offsets,
    targets,
    grid_fine,
    grid_coarse,
    weight_in,
    weight_mid,
    weight_out,
    fine_first,
    fine_second,
    coarse_first,
    coarse_second,
    in_first,
    in_second,
    mid_first,
    mid_second,
    out_first,
    out_second,
):
    channels, sample_rows, sample_cols = grid_fine.shape
    coarse_rows = grid_coarse.shape[1]
    coarse_cols = grid_coarse.shape[2]
    low_in = weight_in.astype(jnp.bfloat16)
    low_mid = weight_mid.astype(jnp.bfloat16)
    low_out = weight_out.astype(jnp.bfloat16)
    top_rows = jnp.concatenate([grid_fine[:, :1, :], grid_coarse[:, :1, :]], axis=2)
    top_rows = shifted(top_rows, "row", -1)
    fine_tall = jnp.concatenate([grid_fine, top_rows[:, :, :sample_cols]], axis=1)
    coarse_tall = jnp.concatenate([grid_coarse, top_rows[:, :, sample_cols:]], axis=1)
    edge_cols = jnp.concatenate([fine_tall[:, :, :1], coarse_tall[:, :, :1]], axis=1)
    edge_cols = shifted(edge_cols, "col", -1)
    fine_ext = jnp.concatenate([fine_tall, edge_cols[:, : sample_rows + 1, :]], axis=2)
    coarse_ext = jnp.concatenate([coarse_tall, edge_cols[:, sample_rows + 1 :, :]], axis=2)
    tables = level_tables(sample_rows, sample_cols, offsets[0, 0, 0], offsets[0, 0, 1])
    features = sample_features(fine_ext, coarse_ext, tables)
    predicted, pre_acts, activations = decoder_forward(features, low_in, low_mid, low_out)
    outputs = predicted.shape[0]
    predicted = predicted.reshape(outputs, sample_rows, sample_cols)
    below = shifted(predicted[:, :1, :], "row", -1)
    beside = shifted(predicted[:, :, :1], "col", -1)
    row_global = lax.axis_index("row") * sample_rows + jnp.arange(sample_rows, dtype=jnp.int32)
    col_global = lax.axis_index("col") * sample_cols + jnp.arange(sample_cols, dtype=jnp.int32)
    row_valid = (row_global < lax.axis_size("row") * sample_rows - 1)[None, :, None]
    col_valid = (col_global < lax.axis_size("col") * sample_cols - 1)[None, None, :]
    row_next = jnp.concatenate([predicted[:, 1:, :], below], axis=1)
    col_next = jnp.concatenate([predicted[:, :, 1:], beside], axis=2)
    value_error = predicted - targets[0]
    row_error = jnp.where(row_valid, row_next - predicted - targets[1], 0.0)
    col_error = jnp.where(col_valid, col_next - predicted - targets[2], 0.0)
    above = shifted(row_error[:, -1:, :], "row", 1)
    before = shifted(col_error[:, :, -1:], "col", 1)
    row_prior = jnp.concatenate([above, row_error[:, :-1, :]], axis=1)
    col_prior = jnp.concatenate([before, col_error[:, :, :-1]], axis=2)
    cotangent = pixel_cotangent(value_error, row_error, row_prior, col_error, col_prior)
    grad_in, grad_mid, grad_out, feature_grad = decoder_backward(
        features,
        pre_acts,
        activations,
        cotangent.reshape(outputs, sample_rows * sample_cols),
        low_in,
        low_mid,
        low_out,
    )
    fine_back, coarse_back = spread_features(feature_grad, tables)
    side_cols = jnp.concatenate(
        [fine_back[:, :, sample_cols:], coarse_back[:, :, coarse_cols:]], axis=1
    )
    side_cols = shifted(side_cols, "col", 1)
    fine_tall_grad = jnp.concatenate(
        [fine_back[:, :, :1] + side_cols[:, : sample_rows + 1, :], fine_back[:, :, 1:sample_cols]],
        axis=2,
    )
    coarse_tall_grad = jnp.concatenate(
        [
            coarse_back[:, :, :1] + side_cols[:, sample_rows + 1 :, :],
            coarse_back[:, :, 1:coarse_cols],
        ],
        axis=2,
    )
    bottom_rows = jnp.concatenate(
        [fine_tall_grad[:, sample_rows:, :], coarse_tall_grad[:, coarse_rows:, :]], axis=2
    )
    bottom_rows = shifted(bottom_rows, "row", 1)
    fine_grad = jnp.concatenate(
        [
            fine_tall_grad[:, :1, :] + bottom_rows[:, :, :sample_cols],
            fine_tall_grad[:, 1:sample_rows, :],
        ],
        axis=1,
    )
    coarse_grad = jnp.concatenate(
        [
            coarse_tall_grad[:, :1, :] + bottom_rows[:, :, sample_cols:],
            coarse_tall_grad[:, 1:coarse_rows, :],
        ],
        axis=1,
    )
    grid_local = jnp.sum(fine_grad * fine_grad) + jnp.sum(coarse_grad * coarse_grad)
    devices = lax.axis_size("row") * lax.axis_size("col")
    grid_entries = (fine_grad.size + coarse_grad.size) * devices
    decoder_entries = weight_in.size + weight_mid.size + weight_out.size
    grad_in, grad_mid, grad_out = lax.psum((grad_in, grad_mid, grad_out), ("row", "col"))
    grid_total = grid_total_sum(grid_local)
    decoder_total = (
        jnp.sum(grad_in * grad_in) + jnp.sum(grad_mid * grad_mid) + jnp.sum(grad_out * grad_out)
    )
    decoder_scale = clip_factor(decoder_total, decoder_entries)
    middle_step = adam_step(grad_mid, mid_first, mid_second, decoder_scale)
    grid_scale = clip_factor(grid_total, grid_entries)
    fine_step = adam_step(fine_grad, fine_first, fine_second, grid_scale)
    coarse_step = adam_step(coarse_grad, coarse_first, coarse_second, grid_scale)
    input_step = adam_step(grad_in, in_first, in_second, decoder_scale)
    output_step = adam_step(grad_out, out_first, out_second, decoder_scale)
    return (fine_step, coarse_step, input_step, middle_step, output_step)


def solution(mesh):
    placed = (
        P("row", "col", None),
        P(None, None, "row", "col"),
        P(None, "row", "col"),
        P(None, "row", "col"),
        P(),
        P(),
        P(),
        P(None, "row", "col"),
        P(None, "row", "col"),
        P(None, "row", "col"),
        P(None, "row", "col"),
        P(),
        P(),
        P(),
        P(),
        P(),
        P(),
    )
    return jax.shard_map(
        shards,
        mesh=mesh,
        in_specs=placed,
        out_specs=(P(None, "row", "col"), P(None, "row", "col"), P(), P(), P()),
        check_vma=False,
    )
```

profile of v0, /device:TPU:0, one launch (start us, length us, event | category | flops | bytes accessed | tf_op | source)
XLA Modules:
  0.0 238.9 jit_solution(828096831755790455)
XLA Ops:
  7.2 0.9 slice.117
  8.2 0.9 copy.59
  9.2 1.3 collective-permute-start
  10.5 1.3 fusion.148
  13.1 0.9 slice_bitcast_fusion.2
  14.0 1.9 collective-permute-done
  16.3 1.1 pad_maximum_fusion
  17.8 1.3 collective-permute-start.1
  19.1 1.8 collective-permute-done.1
  21.6 2.2 fusion.14
  23.8 0.6 convolution_convert_fusion.1
  24.9 0.6 convolution_convert_fusion
  25.6 1.3 fusion.82
  26.9 4.4 %fusion.5 = (bf16[512,4096]{0,1:T(8,128)(2,1)S(1)}, f32[4096,512]{1,0:T(8,128)S(1)}) fusion(f32[1,512,512]{2,1,0:T(8,128)S(1)} %copy-done.11, f32[4096,512]{1,0:T(8,128)S(1)} %fusion.82), kind=kOutput, calls=%fused_computation.10 | convolution fusion | flops 2168717312 | bytes 22020096 | tf_op jit(solution)/shard_map/dot_general | solution.py:80
  31.4 1.2 fusion.125
  32.6 1.3 collective-permute-start.2
  33.9 1.3 collective-permute-start.4
  35.3 3.6 %collective-permute-done.4 = f32[3,32,1]{2,1,0:T(8,128)S(1)} collective-permute-done((f32[3,32,1]{2,1,0:T(8,128)S(1)}, f32[3,32,1]{2,1,0:T(8,128)S(1)}, u32[]{:S(2)}, u32[]{:S(2)}) %collective-permute-start.4) | collective-permute-done | bytes 416 | tf_op jit(solution)/shard_map/ppermute | solution.py:20
  39.1 4.6 %collective-permute-start.5 = (f32[3,32,1]{2,1,0:T(8,128)S(1)}, f32[3,32,1]{2,1,0:T(8,128)S(1)}, u32[]{:S(2)}, u32[]{:S(2)}) collective-permute-start(f32[3,32,1]{2,1,0:T(8,128)S(1)} %slice.167), channel_id=1, source_target_pairs={{0,1},{1,2},{2,3},{4,5},{5,6},{6,7},{8,9},{9,10},{10,11},{12,13},{... | collective-permute-start | bytes 1160 | tf_op jit(solution)/shard_map/ppermute | solution.py:20
  43.8 5.1 %collective-permute-start.3 = (f32[3,1,128]{2,1,0:T(1,128)S(1)}, f32[3,1,128]{2,1,0:T(1,128)S(1)}, u32[]{:S(2)}, u32[]{:S(2)}) collective-permute-start(f32[3,1,128]{2,1,0:T(1,128)S(1)} %slice.163), channel_id=1, source_target_pairs={{0,4},{4,8},{8,12},{12,16},{16,20},{20,24},{24,28},{1,5},{5,9},{9,... | collective-permute-start | bytes 4616 | tf_op jit(solution)/shard_map/ppermute | solution.py:20
  49.0 1.0 collective-permute-done.3
  50.3 3.5 %fusion.1 = bf16[512,4096]{0,1:T(8,128)(2,1)S(1)} fusion(f32[4096,512]{1,0:T(8,128)S(1)} %get-tuple-element.27, bf16[3,4096]{1,0:T(4,128)(2,1)S(1)} %fusion.63, f32[3,512]{1,0:T(4,128)S(1)} %copy-done.8), kind=kOutput, calls=%fused_computation.3 | convolution fusion | flops 31458816 | bytes 12613632 | tf_op jit(solution)/shard_map/dot_general | solution.py:84
  53.8 3.4 %convolution_bitcast_fusion.1 = f32[1,512,512]{2,1,0:T(8,128)} fusion(bf16[512,4096]{0,1:T(8,128)(2,1)S(1)} %fusion.1, f32[4096,512]{1,0:T(8,128)S(1)} %fusion.82), kind=kOutput, calls=%fused_computation.24 | convolution fusion | flops 2157969408 | bytes 13631488 | tf_op jit(solution)/shard_map/dot_general | solution.py:90
  57.3 3.6 %fusion = bf16[512,4096]{0,1:T(8,128)(2,1)S(1)} fusion(f32[4096,512]{1,0:T(8,128)S(1)} %fusion.82, bf16[512,4096]{0,1:T(8,128)(2,1)S(1)} %fusion.1, f32[1,512,512]{2,1,0:T(8,128)S(1)} %copy-done.11), kind=kOutput, calls=%fused_computation.1 | convolution fusion | flops 2166620160 | bytes 17825792 | tf_op jit(solution)/shard_map/dot_general | solution.py:84
  60.9 2.0 copy-done.1
  62.8 1.4 convolution_bitcast_fusion
  64.4 0.4 convolution_bitcast_fusion.3
  65.1 0.7 fusion.147
  66.2 0.8 convolution_bitcast_fusion.2
  67.0 1.2 fusion.56
  68.7 1.3 collective-permute-start.6
  70.0 3.7 %fusion.150 = f32[512,64]{0,1:T(8,128)} fusion(bf16[64,4096]{1,0:T(8,128)(2,1)S(1)} %bitcast_dynamic-update-slice_fusion, bf16[512,4096]{0,1:T(8,128)(2,1)} %copy-done.1), kind=kOutput, calls=%fused_computation.235 | convolution fusion | flops 268435456 | bytes 4849664 | tf_op jit(solution)/shard_map/dot_general | solution.py:90
  74.1 1.2 copy.74
  76.0 0.4 copy.72
  76.6 4.9 %collective-permute-start.7 = (f32[32,1,160]{2,1,0:T(1,128)S(1)}, f32[32,1,160]{2,1,0:T(1,128)S(1)}, u32[]{:S(2)}, u32[]{:S(2)}) collective-permute-start(f32[32,1,160]{2,1,0:T(1,128)S(1)} %fusion.80), channel_id=1, source_target_pairs={{0,4},{4,8},{8,12},{12,16},{16,20},{20,24},{24,28},{1,5},{5,9},{9,... | collective-permute-start | bytes 61448 | tf_op jit(solution)/shard_map/ppermute | solution.py:20
  81.5 2.8 %fusion.149 = f32[3,512]{1,0:T(4,128)S(1)} fusion(bf16[3,4096]{1,0:T(4,128)(2,1)S(1)} %fusion.63, bf16[512,4096]{0,1:T(8,128)(2,1)} %copy-done), kind=kOutput, calls=%fused_computation.234 | convolution fusion | flops 12582912 | bytes 4225024 | tf_op jit(solution)/shard_map/dot_general | solution.py:90
  84.4 0.8 multiply_reduce_fusion.1
  85.3 0.7 multiply_reduce_fusion.3
  87.4 41.9 %all-reduce = (f32[]{:T(128)}, f32[3,512]{1,0:T(4,128)S(1)}) all-reduce(f32[]{:T(128)S(6)} %add.300, f32[3,512]{1,0:T(4,128)S(1)} %fusion.149), channel_id=1, replica_groups=mesh['row'=8,'col'=4] {'row','col'}, use_global_device_ids=true, to_apply=%region_2.3 | all-reduce | flops 1537 | bytes 12296 | tf_op jit(solution)/shard_map/psum | solution.py:146
  129.9 0.7 multiply_reduce_fusion.4
  130.6 1.7 fusion.49
  132.3 2.5 %fusion.29 = f32[32,32,128]{2,1,0:T(8,128)} fusion(f32[32,32,128]{2,1,0:T(8,128)} %param.25, f32[32,32,128]{2,1,0:T(8,128)} %param.24, f32[]{:T(128)S(6)} %min.6, f32[32,33,127]{2,1,0:T(8,128)S(1)} %slice.175, f32[32,33,1]{2,1,0:T(8,128)S(1)} %copy.72, f32[32,1,128]{2,1,0:T(1,128)S(1)} %slice_add_fusion.1), kind=kLoop, calls=%fused_computation.47 | loop fusion | flops 2228224 | bytes 2129924 | tf_op jit(solution)/shard_map/div | solution.py:139
  134.7 86.2 %all-reduce.4.cloned.1.call-done = (f32[512,64]{0,1:T(8,128)}, f32[1,512,512]{2,1,0:T(8,128)}) async-done(((f32[512,64]{0,1:T(8,128)}, f32[1,512,512]{2,1,0:T(8,128)}), (f32[512,64]{0,1:T(8,128)}, f32[1,512,512]{2,1,0:T(8,128)})) %all-reduce.4.cloned.1.call-update) | async-done | bytes 1179664 | tf_op jit(solution)/shard_map/psum | solution.py:250
  220.9 2.1 multiply_reduce_fusion
  223.0 1.5 multiply_reduce_fusion.2
  226.6 0.6 fusion.103
  227.2 3.2 %fusion.24 = f32[1,512,512]{2,1,0:T(8,128)} fusion(f32[1,512,512]{2,1,0:T(8,128)S(1)} %copy-done.2, f32[1,512,512]{2,1,0:T(8,128)} %get-tuple-element.8, f32[1,512,512]{2,1,0:T(8,128)} %param.30, f32[]{:T(128)S(6)} %min.7), kind=kLoop, calls=%fused_computation.39 | loop fusion | flops 3145728 | bytes 4194308 | tf_op jit(solution)/shard_map/div | solution.py:139
  230.4 1.7 fusion.54
  (81 shorter events, 5.7 us)
Async XLA Ops:
  7.2 18.5 %copy-start.3 = (f32[512,64]{0,1:T(8,128)S(1)}, f32[512,64]{0,1:T(8,128)}, u32[]{:S(2)}) copy-start(f32[512,64]{0,1:T(8,128)} %param.21) | copy-start | bytes 393220
  7.2 213.8 %all-reduce.4.cloned.1.call-start = ((), (), s32[]{:S(2)}) async-start(), calls=%async_computation | async-start | bytes 2359296 | tf_op jit(solution)/shard_map/psum | solution.py:250
  9.2 6.8 %collective-permute-start = (f32[32,1,160]{2,1,0:T(1,128)S(1)}, f32[32,1,160]{2,1,0:T(1,128)S(1)}, u32[]{:S(2)}, u32[]{:S(2)}) collective-permute-start(f32[32,1,160]{2,1,0:T(1,128)S(1)} %copy.60), channel_id=1, source_target_pairs={{4,0},{8,4},{12,8},{16,12},{20,16},{24,20},{28,24},{5,1},{9,5},{13... | collective-permute-start | bytes 61448 | tf_op jit(solution)/shard_map/ppermute | solution.py:20
  17.8 3.1 %collective-permute-start.1 = (f32[32,42,1]{1,0,2:T(8,128)S(1)}, f32[32,42,1]{1,0,2:T(8,128)S(1)}, u32[]{:S(2)}, u32[]{:S(2)}) collective-permute-start(f32[32,42,1]{1,0,2:T(8,128)S(1)} %pad_maximum_fusion.7), channel_id=1, source_target_pairs={{1,0},{2,1},{3,2},{5,4},{6,5},{7,6},{9,8},{10,9},{11,10},{13,12},{... | collective-permute-start | bytes 16136 | tf_op jit(solution)/shard_map/ppermute | solution.py:20
  23.8 3.1 %copy-start.11 = (f32[1,512,512]{2,1,0:T(8,128)S(1)}, f32[1,512,512]{2,1,0:T(8,128)}, u32[]{:S(2)}) copy-start(f32[1,512,512]{2,1,0:T(8,128)} %param.22) | copy-start | bytes 3145732
  26.9 4.4 %copy-start.8 = (f32[3,512]{1,0:T(4,128)S(1)}, f32[3,512]{1,0:T(4,128)}, u32[]{:S(2)}) copy-start(f32[3,512]{1,0:T(4,128)} %param.23) | copy-start | bytes 18436
  26.9 12.0 %copy-start.4 = (f32[3,3,32,128]{3,2,1,0:T(8,128)S(1)}, f32[3,3,32,128]{3,2,1,0:T(8,128)}, u32[]{:S(2)}) copy-start(f32[3,3,32,128]{3,2,1,0:T(8,128)} %param.18) | copy-start | bytes 442372
  31.4 22.5 %copy-start = (bf16[512,4096]{0,1:T(8,128)(2,1)}, bf16[512,4096]{0,1:T(8,128)(2,1)S(1)}, u32[]{:S(2)}) copy-start(bf16[512,4096]{0,1:T(8,128)(2,1)S(1)} %get-tuple-element.26) | copy-start | bytes 12582916
  32.6 6.4 %collective-permute-start.2 = (f32[3,1,128]{2,1,0:T(1,128)S(1)}, f32[3,1,128]{2,1,0:T(1,128)S(1)}, u32[]{:S(2)}, u32[]{:S(2)}) collective-permute-start(f32[3,1,128]{2,1,0:T(1,128)S(1)} %slice.162), channel_id=1, source_target_pairs={{4,0},{8,4},{12,8},{16,12},{20,16},{24,20},{28,24},{5,1},{9,5},{13... | collective-permute-start | bytes 4616 | tf_op jit(solution)/shard_map/ppermute | solution.py:20
  33.9 5.0 %collective-permute-start.4 = (f32[3,32,1]{2,1,0:T(8,128)S(1)}, f32[3,32,1]{2,1,0:T(8,128)S(1)}, u32[]{:S(2)}, u32[]{:S(2)}) collective-permute-start(f32[3,32,1]{2,1,0:T(8,128)S(1)} %bitcast.213), channel_id=1, source_target_pairs={{1,0},{2,1},{3,2},{5,4},{6,5},{7,6},{9,8},{10,9},{11,10},{13,12},{... | collective-permute-start | bytes 1160 | tf_op jit(solution)/shard_map/ppermute | solution.py:20
  39.1 9.8 %collective-permute-start.5 = (f32[3,32,1]{2,1,0:T(8,128)S(1)}, f32[3,32,1]{2,1,0:T(8,128)S(1)}, u32[]{:S(2)}, u32[]{:S(2)}) collective-permute-start(f32[3,32,1]{2,1,0:T(8,128)S(1)} %slice.167), channel_id=1, source_target_pairs={{0,1},{1,2},{2,3},{4,5},{5,6},{6,7},{8,9},{9,10},{10,11},{12,13},{... | collective-permute-start | bytes 1160 | tf_op jit(solution)/shard_map/ppermute | solution.py:20
  43.8 6.2 %collective-permute-start.3 = (f32[3,1,128]{2,1,0:T(1,128)S(1)}, f32[3,1,128]{2,1,0:T(1,128)S(1)}, u32[]{:S(2)}, u32[]{:S(2)}) collective-permute-start(f32[3,1,128]{2,1,0:T(1,128)S(1)} %slice.163), channel_id=1, source_target_pairs={{0,4},{4,8},{8,12},{12,16},{16,20},{20,24},{24,28},{1,5},{5,9},{9,... | collective-permute-start | bytes 4616 | tf_op jit(solution)/shard_map/ppermute | solution.py:20
  60.8 2.0 copy-start.1
  68.7 6.9 %collective-permute-start.6 = (f32[32,42,1]{1,0,2:T(8,128)S(1)}, f32[32,42,1]{1,0,2:T(8,128)S(1)}, u32[]{:S(2)}, u32[]{:S(2)}) collective-permute-start(f32[32,42,1]{1,0,2:T(8,128)S(1)} %pad_maximum_fusion.8), channel_id=1, source_target_pairs={{0,1},{1,2},{2,3},{4,5},{5,6},{6,7},{8,9},{9,10},{10,11},{12,13},{... | collective-permute-start | bytes 16136 | tf_op jit(solution)/shard_map/ppermute | solution.py:20
  73.6 57.0 %copy-start.5 = (f32[32,8,32]{2,1,0:T(8,128)S(1)}, f32[32,8,32]{2,1,0:T(8,128)}, u32[]{:S(2)}) copy-start(f32[32,8,32]{2,1,0:T(8,128)} %param.27) | copy-start | bytes 98308
  75.7 150.9 %copy-start.9 = (f32[3,512]{1,0:T(4,128)S(1)}, f32[3,512]{1,0:T(4,128)}, u32[]{:S(2)}) copy-start(f32[3,512]{1,0:T(4,128)} %param.33) | copy-start | bytes 18436
  75.7 150.9 %copy-start.10 = (f32[3,512]{1,0:T(4,128)S(1)}, f32[3,512]{1,0:T(4,128)}, u32[]{:S(2)}) copy-start(f32[3,512]{1,0:T(4,128)} %param.32) | copy-start | bytes 18436
  75.7 151.5 %copy-start.2 = (f32[1,512,512]{2,1,0:T(8,128)S(1)}, f32[1,512,512]{2,1,0:T(8,128)}, u32[]{:S(2)}) copy-start(f32[1,512,512]{2,1,0:T(8,128)} %param.31) | copy-start | bytes 3145732
  76.5 153.9 %copy-start.6 = (f32[512,64]{0,1:T(8,128)S(1)}, f32[512,64]{0,1:T(8,128)}, u32[]{:S(2)}) copy-start(f32[512,64]{0,1:T(8,128)} %param.29) | copy-start | bytes 393220
  76.5 153.8 %copy-start.7 = (f32[512,64]{0,1:T(8,128)S(1)}, f32[512,64]{0,1:T(8,128)}, u32[]{:S(2)}) copy-start(f32[512,64]{0,1:T(8,128)} %param.28) | copy-start | bytes 393220
  76.6 7.7 %collective-permute-start.7 = (f32[32,1,160]{2,1,0:T(1,128)S(1)}, f32[32,1,160]{2,1,0:T(1,128)S(1)}, u32[]{:S(2)}, u32[]{:S(2)}) collective-permute-start(f32[32,1,160]{2,1,0:T(1,128)S(1)} %fusion.80), channel_id=1, source_target_pairs={{0,4},{4,8},{8,12},{12,16},{16,20},{20,24},{24,28},{1,5},{5,9},{9,... | collective-permute-start | bytes 61448 | tf_op jit(solution)/shard_map/ppermute | solution.py:20
Sparse Core Ops, SparseCore 0:
  87.5 133.4 all-reduce.3
where the time goes:
time: 240 us; the launch traced here: 239 us
  waiting for transfers between devices  94.6 us (39%)
  blocking collectives  41.9 us (17%)
  matrix products  31.7 us (13%)
  starting transfers between devices  21.1 us (9%)
  between operations  19.8 us (8%)
  other arithmetic  17.7 us (7%)
  local copies, waits for them, and re-layouts  12.2 us (5%)
    psum x1, waiting for transfers between devices, shards(): lax.psum((grad_in, grad_mid, grad_out), ('row', 'col'))  86.2 us
    psum x1, blocking collectives, grid_total_sum(): return lax.psum(grid_local, ('row', 'col'))  41.9 us
    ppermute x8, starting transfers between devices, shifted(): return lax.ppermute(block, axis, route)  21.1 us
    dot_general x3, matrix products, contract_cols(): lax.dot_general(former, latter, (((1,), (1,)), ((), ())), preferred_eleme...  9.93 us
    div x5, other arithmetic, adam_step(): new_one / (1.0 - BETA_ONE ** ADAM_STEP)  9.62 us
    dot_general x3, matrix products, contract_rows(): lax.dot_general(former, latter, (((0,), (0,)), ((), ())), preferred_eleme...  8.45 us
    ppermute x8, waiting for transfers between devices, shifted(): return lax.ppermute(block, axis, route)  8.35 us
    dot_general x3, matrix products, matmul(): return jnp.dot(former, latter, preferred_element_type=jnp.float32)  6.85 us
  transfers between devices with their start and end apart: 9, of which 6 were waited for; matrix products, arithmetic and copies ran while one was open for 7% of the time, Pallas kernels for 0%

commit v1 on v0

--- a/solution.py
+++ b/solution.py
@@ -2,6 +2,7 @@
 import jax.numpy as jnp
 from jax import lax
 from jax.sharding import PartitionSpec as P
+from jax.lax import psum
 
 SUB = 4
 RATIO = 4
@@ -143,7 +144,7 @@
 
 
 def grid_total_sum(grid_local):
-    return lax.psum(grid_local, ("row", "col"))
+    return psum(psum(grid_local, "col"), "row")
 
 
 def shards(

time: 240 us -> 282 us (1.18)
  blocking collectives: 41.9 us -> 68.3 us
  waiting for transfers between devices: 94.6 us -> 108 us
    psum x1 -> x3, blocking collectives: 41.9 us -> 68.3 us  [the longest x1 40.3 us: shards(): lax.psum((grad_in, grad_mid, grad_out), ('row', 'col'))]
    psum x1, waiting for transfers between devices: 86.2 us -> 98.7 us  [shards(): lax.psum((grad_in, grad_mid, grad_out), ('row', 'col'))]
    unnamed x32 -> x28, local copies, waits for them, and re-layouts: 4.27 us -> 6.13 us
  transfers between devices with their start and end apart: 9 -> 9, of which waited for: 6 -> 6; matrix products, arithmetic and copies ran while one was open for 7% -> 5% of each run, Pallas kernels for 0% -> 0%
where the time goes in v1:
time: 282 us; the launch traced here: 281 us
  waiting for transfers between devices  108 us (38%)
  blocking collectives  68.3 us (24%)
  matrix products  31.7 us (11%)
  starting transfers between devices  21.5 us (8%)
  between operations  19.8 us (7%)
  other arithmetic  18.4 us (7%)
  local copies, waits for them, and re-layouts  12.5 us (4%)
    psum x1, waiting for transfers between devices, shards(): lax.psum((grad_in, grad_mid, grad_out), ('row', 'col'))  98.7 us
    psum x1, blocking collectives, shards(): lax.psum((grad_in, grad_mid, grad_out), ('row', 'col'))  40.3 us
    psum x2, blocking collectives, grid_total_sum(): return psum(psum(grid_local, 'col'), 'row')  28 us
    ppermute x8, starting transfers between devices, shifted(): return lax.ppermute(block, axis, route)  21.4 us
    dot_general x3, matrix products, contract_cols(): lax.dot_general(former, latter, (((1,), (1,)), ((), ())), preferred_eleme...  9.94 us
    div x5, other arithmetic, adam_step(): new_one / (1.0 - BETA_ONE ** ADAM_STEP)  9.7 us
    ppermute x8, waiting for transfers between devices, shifted(): return lax.ppermute(block, axis, route)  9.67 us
    dot_general x3, matrix products, contract_rows(): lax.dot_general(former, latter, (((0,), (0,)), ((), ())), preferred_eleme...  8.46 us
  transfers between devices with their start and end apart: 9, of which 6 were waited for; matrix products, arithmetic and copies ran while one was open for 5% of the time, Pallas kernels for 0%

profile of v1, /device:TPU:0, one launch (start us, length us, event | category | flops | bytes accessed | tf_op | source)
XLA Modules:
  0.0 280.6 jit_solution(12101694119807830584)
XLA Ops:
  7.2 1.0 copy.59
  8.2 0.9 slice.117
  9.2 1.3 collective-permute-start
  10.5 1.3 fusion.148
  13.1 0.9 slice_bitcast_fusion.2
  14.0 1.9 collective-permute-done
  16.3 1.1 pad_maximum_fusion
  17.8 1.3 collective-permute-start.1
  19.1 1.8 collective-permute-done.1
  21.6 2.2 fusion.14
  24.9 0.6 convolution_convert_fusion
  25.6 1.3 fusion.82
  26.9 4.4 %fusion.5 = (bf16[512,4096]{0,1:T(8,128)(2,1)S(1)}, f32[4096,512]{1,0:T(8,128)S(1)}) fusion(f32[1,512,512]{2,1,0:T(8,128)S(1)} %copy-done.9, f32[4096,512]{1,0:T(8,128)S(1)} %fusion.82), kind=kOutput, calls=%fused_computation.10 | convolution fusion | flops 2168717312 | bytes 22020096 | tf_op jit(solution)/shard_map/dot_general | solution.py:81
  31.4 1.2 fusion.125
  32.6 1.3 collective-permute-start.4
  33.9 1.3 collective-permute-start.2
  35.3 2.3 collective-permute-done.4
  37.6 2.6 collective-permute-done.2
  40.4 3.5 %collective-permute-start.5 = (f32[3,32,1]{2,1,0:T(8,128)S(1)}, f32[3,32,1]{2,1,0:T(8,128)S(1)}, u32[]{:S(2)}, u32[]{:S(2)}) collective-permute-start(f32[3,32,1]{2,1,0:T(8,128)S(1)} %slice.167), channel_id=1, source_target_pairs={{0,1},{1,2},{2,3},{4,5},{5,6},{6,7},{8,9},{9,10},{10,11},{12,13},{... | collective-permute-start | bytes 1160 | tf_op jit(solution)/shard_map/ppermute | solution.py:21
  44.1 4.7 %collective-permute-start.3 = (f32[3,1,128]{2,1,0:T(1,128)S(1)}, f32[3,1,128]{2,1,0:T(1,128)S(1)}, u32[]{:S(2)}, u32[]{:S(2)}) collective-permute-start(f32[3,1,128]{2,1,0:T(1,128)S(1)} %slice.163), channel_id=1, source_target_pairs={{0,4},{4,8},{8,12},{12,16},{16,20},{20,24},{24,28},{1,5},{5,9},{9,... | collective-permute-start | bytes 4616 | tf_op jit(solution)/shard_map/ppermute | solution.py:21
  48.9 1.0 collective-permute-done.3
  50.1 3.5 %fusion.1 = bf16[512,4096]{0,1:T(8,128)(2,1)S(1)} fusion(f32[4096,512]{1,0:T(8,128)S(1)} %get-tuple-element.25, bf16[3,4096]{1,0:T(4,128)(2,1)S(1)} %fusion.63, f32[3,512]{1,0:T(4,128)S(1)} %copy-done.6), kind=kOutput, calls=%fused_computation.3 | convolution fusion | flops 31458816 | bytes 12613632 | tf_op jit(solution)/shard_map/dot_general | solution.py:85
  53.7 3.4 %convolution_bitcast_fusion.1 = f32[1,512,512]{2,1,0:T(8,128)} fusion(bf16[512,4096]{0,1:T(8,128)(2,1)S(1)} %fusion.1, f32[4096,512]{1,0:T(8,128)S(1)} %fusion.82), kind=kOutput, calls=%fused_computation.24 | convolution fusion | flops 2157969408 | bytes 13631488 | tf_op jit(solution)/shard_map/dot_general | solution.py:91
  57.1 3.6 %fusion = bf16[512,4096]{0,1:T(8,128)(2,1)S(1)} fusion(f32[4096,512]{1,0:T(8,128)S(1)} %fusion.82, bf16[512,4096]{0,1:T(8,128)(2,1)S(1)} %fusion.1, f32[1,512,512]{2,1,0:T(8,128)S(1)} %copy-done.9), kind=kOutput, calls=%fused_computation.1 | convolution fusion | flops 2166620160 | bytes 17825792 | tf_op jit(solution)/shard_map/dot_general | solution.py:85
  60.7 2.0 copy-done.1
  62.7 1.4 convolution_bitcast_fusion
  64.0 0.9 slice_bitcast_fusion
  65.0 0.8 convolution_bitcast_fusion.2
  65.8 1.2 fusion.56
  67.4 1.1 copy.92
  69.7 3.9 %collective-permute-start.6 = (f32[32,42,1]{1,0,2:T(8,128)S(1)}, f32[32,42,1]{1,0,2:T(8,128)S(1)}, u32[]{:S(2)}, u32[]{:S(2)}) collective-permute-start(f32[32,42,1]{1,0,2:T(8,128)S(1)} %pad_maximum_fusion.8), channel_id=1, source_target_pairs={{0,1},{1,2},{2,3},{4,5},{5,6},{6,7},{8,9},{9,10},{10,11},{12,13},{... | collective-permute-start | bytes 16136 | tf_op jit(solution)/shard_map/ppermute | solution.py:21
  73.7 3.7 %fusion.150 = f32[512,64]{0,1:T(8,128)} fusion(bf16[64,4096]{1,0:T(8,128)(2,1)S(1)} %bitcast_dynamic-update-slice_fusion, bf16[512,4096]{0,1:T(8,128)(2,1)} %copy-done.1), kind=kOutput, calls=%fused_computation.235 | convolution fusion | flops 268435456 | bytes 4849664 | tf_op jit(solution)/shard_map/dot_general | solution.py:91
  79.3 4.1 %collective-permute-start.7 = (f32[32,1,160]{2,1,0:T(1,128)S(1)}, f32[32,1,160]{2,1,0:T(1,128)S(1)}, u32[]{:S(2)}, u32[]{:S(2)}) collective-permute-start(f32[32,1,160]{2,1,0:T(1,128)S(1)} %fusion.80), channel_id=1, source_target_pairs={{0,4},{4,8},{8,12},{12,16},{16,20},{20,24},{24,28},{1,5},{5,9},{9,... | collective-permute-start | bytes 61448 | tf_op jit(solution)/shard_map/ppermute | solution.py:21
  83.5 2.8 %fusion.149 = f32[3,512]{1,0:T(4,128)S(1)} fusion(bf16[3,4096]{1,0:T(4,128)(2,1)S(1)} %fusion.63, bf16[512,4096]{0,1:T(8,128)(2,1)} %copy-done), kind=kOutput, calls=%fused_computation.234 | convolution fusion | flops 12582912 | bytes 4225024 | tf_op jit(solution)/shard_map/dot_general | solution.py:91
  86.3 40.3 %psum.39 = f32[3,512]{1,0:T(4,128)S(1)} all-reduce(f32[3,512]{1,0:T(4,128)S(1)} %fusion.149), channel_id=1, replica_groups=mesh['row'=8,'col'=4] {'row','col'}, use_global_device_ids=true, to_apply=%region_8.9 | all-reduce | flops 1536 | bytes 12288 | tf_op jit(solution)/shard_map/psum | solution.py:251
  126.7 1.4 multiply_reduce_fusion.3
  128.1 0.8 multiply_reduce_fusion.1
  130.3 6.5 %psum.35 = f32[]{:T(128)} all-reduce(f32[]{:T(128)S(6)} %add.302), channel_id=1, replica_groups=mesh['row'=8,'col'=4] {'col'}, use_global_device_ids=true, to_apply=%region_2.3 | all-reduce | flops 1 | bytes 8 | tf_op jit(solution)/shard_map/psum | solution.py:147
  136.8 0.7 multiply_reduce_fusion.4
  137.4 21.5 %psum.36 = f32[]{:T(128)} all-reduce(f32[]{:T(128)} %psum.35), channel_id=1, replica_groups=mesh['row'=8,'col'=4] {'row'}, use_global_device_ids=true, to_apply=%region_3.4 | all-reduce | flops 1 | bytes 8 | tf_op jit(solution)/shard_map/psum | solution.py:147
  159.6 1.8 fusion.49
  161.4 2.3 fusion.29
  163.7 98.7 %all-reduce.3.cloned.1.call-done = (f32[512,64]{0,1:T(8,128)}, f32[1,512,512]{2,1,0:T(8,128)}) async-done(((f32[512,64]{0,1:T(8,128)}, f32[1,512,512]{2,1,0:T(8,128)}), (f32[512,64]{0,1:T(8,128)}, f32[1,512,512]{2,1,0:T(8,128)})) %all-reduce.3.cloned.1.call-update) | async-done | bytes 1179664 | tf_op jit(solution)/shard_map/psum | solution.py:251
  262.4 2.1 multiply_reduce_fusion
  264.5 1.5 multiply_reduce_fusion.2
  268.1 0.6 fusion.103
  268.7 3.2 %fusion.24 = f32[1,512,512]{2,1,0:T(8,128)} fusion(f32[1,512,512]{2,1,0:T(8,128)S(1)} %copy-done.2, f32[1,512,512]{2,1,0:T(8,128)} %get-tuple-element.6, f32[1,512,512]{2,1,0:T(8,128)} %param.30, f32[]{:T(128)S(6)} %min.7), kind=kLoop, calls=%fused_computation.39 | loop fusion | flops 3145728 | bytes 4194308 | tf_op jit(solution)/shard_map/div | solution.py:140
  271.9 1.8 fusion.54
  (79 shorter events, 7.3 us)
Async XLA Ops:
  7.2 18.4 %copy-start.3 = (f32[512,64]{0,1:T(8,128)S(1)}, f32[512,64]{0,1:T(8,128)}, u32[]{:S(2)}) copy-start(f32[512,64]{0,1:T(8,128)} %param.21) | copy-start | bytes 393220
  7.2 255.3 %all-reduce.3.cloned.1.call-start = ((), (), s32[]{:S(2)}) async-start(), calls=%async_computation | async-start | bytes 2359296 | tf_op jit(solution)/shard_map/psum | solution.py:251
  9.2 6.8 %collective-permute-start = (f32[32,1,160]{2,1,0:T(1,128)S(1)}, f32[32,1,160]{2,1,0:T(1,128)S(1)}, u32[]{:S(2)}, u32[]{:S(2)}) collective-permute-start(f32[32,1,160]{2,1,0:T(1,128)S(1)} %copy.60), channel_id=1, source_target_pairs={{4,0},{8,4},{12,8},{16,12},{20,16},{24,20},{28,24},{5,1},{9,5},{13... | collective-permute-start | bytes 61448 | tf_op jit(solution)/shard_map/ppermute | solution.py:21
  17.8 3.1 %collective-permute-start.1 = (f32[32,42,1]{1,0,2:T(8,128)S(1)}, f32[32,42,1]{1,0,2:T(8,128)S(1)}, u32[]{:S(2)}, u32[]{:S(2)}) collective-permute-start(f32[32,42,1]{1,0,2:T(8,128)S(1)} %pad_maximum_fusion.7), channel_id=1, source_target_pairs={{1,0},{2,1},{3,2},{5,4},{6,5},{7,6},{9,8},{10,9},{11,10},{13,12},{... | collective-permute-start | bytes 16136 | tf_op jit(solution)/shard_map/ppermute | solution.py:21
  23.8 3.1 %copy-start.9 = (f32[1,512,512]{2,1,0:T(8,128)S(1)}, f32[1,512,512]{2,1,0:T(8,128)}, u32[]{:S(2)}) copy-start(f32[1,512,512]{2,1,0:T(8,128)} %param.22) | copy-start | bytes 3145732
  26.9 4.5 %copy-start.6 = (f32[3,512]{1,0:T(4,128)S(1)}, f32[3,512]{1,0:T(4,128)}, u32[]{:S(2)}) copy-start(f32[3,512]{1,0:T(4,128)} %param.23) | copy-start | bytes 18436
  26.9 13.3 %copy-start.5 = (f32[3,3,32,128]{3,2,1,0:T(8,128)S(1)}, f32[3,3,32,128]{3,2,1,0:T(8,128)}, u32[]{:S(2)}) copy-start(f32[3,3,32,128]{3,2,1,0:T(8,128)} %param.18) | copy-start | bytes 442372
  31.4 22.3 %copy-start = (bf16[512,4096]{0,1:T(8,128)(2,1)}, bf16[512,4096]{0,1:T(8,128)(2,1)S(1)}, u32[]{:S(2)}) copy-start(bf16[512,4096]{0,1:T(8,128)(2,1)S(1)} %get-tuple-element.24) | copy-start | bytes 12582916
  32.6 5.0 %collective-permute-start.4 = (f32[3,32,1]{2,1,0:T(8,128)S(1)}, f32[3,32,1]{2,1,0:T(8,128)S(1)}, u32[]{:S(2)}, u32[]{:S(2)}) collective-permute-start(f32[3,32,1]{2,1,0:T(8,128)S(1)} %bitcast.213), channel_id=1, source_target_pairs={{1,0},{2,1},{3,2},{5,4},{6,5},{7,6},{9,8},{10,9},{11,10},{13,12},{... | collective-permute-start | bytes 1160 | tf_op jit(solution)/shard_map/ppermute | solution.py:21
  33.9 6.4 %collective-permute-start.2 = (f32[3,1,128]{2,1,0:T(1,128)S(1)}, f32[3,1,128]{2,1,0:T(1,128)S(1)}, u32[]{:S(2)}, u32[]{:S(2)}) collective-permute-start(f32[3,1,128]{2,1,0:T(1,128)S(1)} %slice.162), channel_id=1, source_target_pairs={{4,0},{8,4},{12,8},{16,12},{20,16},{24,20},{28,24},{5,1},{9,5},{13... | collective-permute-start | bytes 4616 | tf_op jit(solution)/shard_map/ppermute | solution.py:21
  40.4 8.3 %collective-permute-start.5 = (f32[3,32,1]{2,1,0:T(8,128)S(1)}, f32[3,32,1]{2,1,0:T(8,128)S(1)}, u32[]{:S(2)}, u32[]{:S(2)}) collective-permute-start(f32[3,32,1]{2,1,0:T(8,128)S(1)} %slice.167), channel_id=1, source_target_pairs={{0,1},{1,2},{2,3},{4,5},{5,6},{6,7},{8,9},{9,10},{10,11},{12,13},{... | collective-permute-start | bytes 1160 | tf_op jit(solution)/shard_map/ppermute | solution.py:21
  44.1 5.8 %collective-permute-start.3 = (f32[3,1,128]{2,1,0:T(1,128)S(1)}, f32[3,1,128]{2,1,0:T(1,128)S(1)}, u32[]{:S(2)}, u32[]{:S(2)}) collective-permute-start(f32[3,1,128]{2,1,0:T(1,128)S(1)} %slice.163), channel_id=1, source_target_pairs={{0,4},{4,8},{8,12},{12,16},{16,20},{20,24},{24,28},{1,5},{5,9},{9,... | collective-permute-start | bytes 4616 | tf_op jit(solution)/shard_map/ppermute | solution.py:21
  60.7 2.0 copy-start.1
  69.7 8.7 %collective-permute-start.6 = (f32[32,42,1]{1,0,2:T(8,128)S(1)}, f32[32,42,1]{1,0,2:T(8,128)S(1)}, u32[]{:S(2)}, u32[]{:S(2)}) collective-permute-start(f32[32,42,1]{1,0,2:T(8,128)S(1)} %pad_maximum_fusion.8), channel_id=1, source_target_pairs={{0,1},{1,2},{2,3},{4,5},{5,6},{6,7},{8,9},{9,10},{10,11},{12,13},{... | collective-permute-start | bytes 16136 | tf_op jit(solution)/shard_map/ppermute | solution.py:21
  77.3 84.1 %copy-start.4 = (f32[32,32,128]{2,1,0:T(8,128)S(1)}, f32[32,32,128]{2,1,0:T(8,128)}, u32[]{:S(2)}) copy-start(f32[32,32,128]{2,1,0:T(8,128)} %param.25) | copy-start | bytes 1572868
  78.5 189.6 %copy-start.7 = (f32[3,512]{1,0:T(4,128)S(1)}, f32[3,512]{1,0:T(4,128)}, u32[]{:S(2)}) copy-start(f32[3,512]{1,0:T(4,128)} %param.33) | copy-start | bytes 18436
  78.5 189.6 %copy-start.8 = (f32[3,512]{1,0:T(4,128)S(1)}, f32[3,512]{1,0:T(4,128)}, u32[]{:S(2)}) copy-start(f32[3,512]{1,0:T(4,128)} %param.32) | copy-start | bytes 18436
  78.5 190.2 %copy-start.2 = (f32[1,512,512]{2,1,0:T(8,128)S(1)}, f32[1,512,512]{2,1,0:T(8,128)}, u32[]{:S(2)}) copy-start(f32[1,512,512]{2,1,0:T(8,128)} %param.31) | copy-start | bytes 3145732
  79.3 47.2 %collective-permute-start.7 = (f32[32,1,160]{2,1,0:T(1,128)S(1)}, f32[32,1,160]{2,1,0:T(1,128)S(1)}, u32[]{:S(2)}, u32[]{:S(2)}) collective-permute-start(f32[32,1,160]{2,1,0:T(1,128)S(1)} %fusion.80), channel_id=1, source_target_pairs={{0,4},{4,8},{8,12},{12,16},{16,20},{20,24},{24,28},{1,5},{5,9},{9,... | collective-permute-start | bytes 61448 | tf_op jit(solution)/shard_map/ppermute | solution.py:21
Sparse Core Ops, SparseCore 0:
  130.4 131.9 all-reduce.2
